TPU v7x, 8 devices: a whole 2x2x1 slice. The times are simulated.
8 devices in a mesh: dp: 2 (over y, z), tp: 4 (over x, core).
Axes of the slice: x: 2, y: 2, z: 1, core: 2. Of those that a mesh axis runs over, the one named last changes fastest.
Arguments:
- x: bfloat16 [1792, 5376], P(('dp', 'tp')), parts along dimension 0
- w_gate: bfloat16 [5376, 21504], P(None, 'tp')
- w_up: bfloat16 [5376, 21504], P(None, 'tp')
- w_down: bfloat16 [21504, 5376], P('tp')
Outputs:
- output: bfloat16 [1792, 5376], P(('dp', 'tp')), parts along dimension 0
There are 2 independent parts. A program takes and returns all parts, laid end to end along the dimension named above; an argument that names none is the same for every part.
All inputs are finite; a program needn't handle non-finite values.
Results may differ from a plain program's by a relative error of at most 0.016.
Values are sent between devices in bfloat16 or wider.
A program may use at most 2 GiB of HBM per device.

v0:
```python
import jax
import jax.numpy as jnp
from jax import lax
from jax.sharding import PartitionSpec as P


def solution(mesh):
    def step(x, w_gate, w_up, w_down):
        rows = lax.all_gather(x, "tp", axis=0, tiled=True)
        gate = jnp.dot(rows, w_gate, preferred_element_type=jnp.float32)
        up = jnp.dot(rows, w_up, preferred_element_type=jnp.float32)
        hidden = (jax.nn.gelu(gate) * up).astype(jnp.bfloat16)
        term = jnp.dot(hidden, w_down, preferred_element_type=jnp.float32).astype(jnp.bfloat16)
        return lax.psum_scatter(term, "tp", scatter_dimension=0, tiled=True)

    return jax.shard_map(
        step,
        mesh=mesh,
        in_specs=(P(("dp", "tp"), None), P(None, "tp"), P(None, "tp"), P("tp", None)),
        out_specs=P(("dp", "tp"), None),
        check_vma=False,
    )
```

profile of v0, /device:TPU:0, one launch (start us, length us, event | category | flops | bytes accessed | tf_op | source)
XLA Modules:
  0.0 340.1 jit_solution(2681072373956101404)
XLA Ops:
  6.5 0.0 all-gather.2.cloned.1.call-start
  6.5 0.7 all-gather.2.cloned.1.call-update
  7.3 0.0 reduce-scatter.2.cloned.1.call-start
  7.3 67.3 %all-gather.2.cloned.1.call-done = bf16[896,5376]{1,0:T(8,128)(2,1)} async-done(((bf16[224,5376]{1,0:T(8,128)(2,1)}), bf16[896,5376]{1,0:T(8,128)(2,1)}) %all-gather.2.cloned.1.call-update) | async-done | bytes 9633808 | tf_op jit(solution)/shard_map/all_gather | solution.py:9
  74.6 0.0 copy-start
  74.6 63.6 %fusion.9 = f32[896,5376]{1,0:T(8,128)} fusion(bf16[896,5376]{1,0:T(8,128)(2,1)} %all-gather.2.cloned.1.call-done, bf16[5376,5376]{1,0:T(8,128)(2,1)} %param.5), kind=kOutput, calls=%fused_computation.11 | convolution fusion | flops 51791265792 | bytes 86704128 | tf_op jit(solution)/shard_map/dot_general | solution.py:10
  138.2 0.0 copy-done
  138.2 61.2 %fusion.8 = bf16[896,5376]{1,0:T(8,128)(2,1)} fusion(f32[896,5376]{1,0:T(8,128)} %fusion.9, bf16[896,5376]{1,0:T(8,128)(2,1)S(1)} %copy-done, bf16[5376,5376]{1,0:T(8,128)(2,1)} %param.6), kind=kOutput, calls=%fused_computation.9 | convolution fusion | flops 51839434752 | bytes 96337920 | tf_op jit(solution)/shard_map/dot_general | solution.py:11
  199.4 61.0 %convolution_convert_fusion = bf16[896,5376]{1,0:T(8,128)(2,1)} fusion(bf16[896,5376]{1,0:T(8,128)(2,1)} %fusion.8, bf16[5376,5376]{1,0:T(8,128)(2,1)} %param.7), kind=kOutput, calls=%fused_computation.10 | convolution fusion | flops 51796082688 | bytes 77070336 | tf_op jit(solution)/shard_map/dot_general | solution.py:13
  260.4 0.0 reduce-scatter.2.cloned.1.call-update
  260.4 72.8 %reduce-scatter.2.cloned.1.call-done = bf16[224,5376]{1,0:T(8,128)(2,1)} async-done(((bf16[896,5376]{1,0:T(8,128)(2,1)}), bf16[224,5376]{1,0:T(8,128)(2,1)}) %reduce-scatter.2.cloned.1.call-update) | async-done | bytes 2408464 | tf_op jit(solution)/shard_map/reduce_scatter | solution.py:14
Async XLA Ops:
  6.5 68.1 %all-gather.2.cloned.1.call-start = ((), (), s32[]{:S(2)}) async-start(), calls=%async_computation.1 | async-start | bytes 12042240 | tf_op jit(solution)/shard_map/all_gather | solution.py:9
  7.3 326.0 %reduce-scatter.2.cloned.1.call-start = ((), (), s32[]{:S(2)}) async-start(), calls=%async_computation.2 | async-start | bytes 12042240 | tf_op jit(solution)/shard_map/reduce_scatter | solution.py:14
  74.6 63.6 %copy-start = (bf16[896,5376]{1,0:T(8,128)(2,1)S(1)}, bf16[896,5376]{1,0:T(8,128)(2,1)}, u32[]{:S(2)}) copy-start(bf16[896,5376]{1,0:T(8,128)(2,1)} %all-gather.2.cloned.1.call-done) | copy-start | bytes 28901380
Sparse Core Ops, SparseCore 0:
  8.9 65.7 all-gather.1
  260.6 72.6 reduce-scatter.1
where the time goes:
time: 340 us
  matrix products  186 us (55%)
  waiting for transfers between devices  141 us (41%)
  between operations  13.4 us (4%)
    reduce_scatter x1, waiting for transfers between devices, step(): return lax.psum_scatter(term, 'tp', scatter_dimension=0, tiled=True)  72.8 us
    all_gather x1, waiting for transfers between devices, step(): rows = lax.all_gather(x, 'tp', axis=0, tiled=True)  67.3 us
    dot_general x1, matrix products, step(): gate = jnp.dot(rows, w_gate, preferred_element_type=jnp.float32)  63.6 us
    dot_general x1, matrix products, step(): up = jnp.dot(rows, w_up, preferred_element_type=jnp.float32)  61.2 us
    dot_general x1, matrix products, step(): jnp.dot(hidden, w_down, preferred_element_type=jnp.float32)  61 us
  transfers between devices with their start and end apart: 2, of which 2 were waited for; matrix products, arithmetic and copies ran while one was open for 0% of the time, Pallas kernels for 0%

commit v1 on v0

v1 whole, which is shorter than its diff:
```python
import functools

import jax
import jax.numpy as jnp
from jax import lax
from jax.experimental import pallas as pl
from jax.experimental.pallas import tpu as pltpu
from jax.sharding import PartitionSpec as P

NT = 256
UN = 3
VMEM_LIMIT = 67043328
MESH = pl.DeviceIdType.MESH


def dot(a, b):
    return jnp.dot(a, b, preferred_element_type=jnp.float32)


def kernel(
    x_ref, wg_ref, wu_ref, wd_ref, y_ref,
    xb, hb, wr, gs, us, sib_in, link_in,
    wsem, xsem, xsib_send, xsib_recv, xlink_send, xlink_recv, fwd_send, fwd_recv,
    sib_send, sib_recv, link_send, link_recv, ysem,
):
    rows, depth = x_ref.shape
    two = 2 * rows
    tiles = depth // NT
    trips = tiles // UN
    wide = UN * NT
    pieces = xlink_recv.shape[0]
    prow = rows // pieces

    me = lax.axis_index("tp")
    sib = me + 1 - 2 * lax.rem(me, 2)
    far = lax.rem(me + 2, 4)

    def al(v, m):
        return pl.multiple_of(v, m)

    def tile_copy(w, half, k, tile):
        return pltpu.make_async_copy(
            w.at[:, pl.ds(al(tile * NT, NT), NT)], wr.at[half, k], wsem.at[half, k]
        )

    def fetch_gu(t, pair):
        for k in range(UN):
            tile_copy(wg_ref, 2 * pair, k, t * UN + k).start()
            tile_copy(wu_ref, 2 * pair + 1, k, t * UN + k).start()

    def wait_w(half, k):
        tile_copy(wg_ref, half, k, 0).wait()

    def fetch_d(t, half):
        for k in range(UN):
            tile_copy(wd_ref, half, k, t * UN + k).start()

    def x_sib():
        return pltpu.make_async_remote_copy(
            src_ref=x_ref, dst_ref=xb.at[pl.ds(rows, rows), :],
            send_sem=xsib_send, recv_sem=xsib_recv,
            device_id={"tp": sib}, device_id_type=MESH,
        )

    def x_link(c):
        return pltpu.make_async_remote_copy(
            src_ref=x_ref.at[pl.ds(c * prow, prow), :],
            dst_ref=xb.at[pl.ds(two + c * prow, prow), :],
            send_sem=xlink_send.at[c], recv_sem=xlink_recv.at[c],
            device_id={"tp": far}, device_id_type=MESH,
        )

    def x_fwd(c):
        return pltpu.make_async_remote_copy(
            src_ref=xb.at[pl.ds(two + c * prow, prow), :],
            dst_ref=xb.at[pl.ds(two + rows + c * prow, prow), :],
            send_sem=fwd_send.at[c], recv_sem=fwd_recv.at[c],
            device_id={"tp": sib}, device_id_type=MESH,
        )

    def t_sib(r, j):
        return pltpu.make_async_remote_copy(
            src_ref=xb.at[pl.ds(al(r * two, two), rows), pl.ds(al(j * wide, wide), wide)],
            dst_ref=sib_in.at[:, pl.ds(al(j * wide, wide), wide)],
            send_sem=sib_send.at[r, j], recv_sem=sib_recv.at[r, j],
            device_id={"tp": sib}, device_id_type=MESH,
        )

    def t_link(j):
        return pltpu.make_async_remote_copy(
            src_ref=xb.at[pl.ds(rows, rows), pl.ds(al(j * wide, wide), wide)],
            dst_ref=link_in.at[:, pl.ds(al(j * wide, wide), wide)],
            send_sem=link_send.at[j], recv_sem=link_recv.at[j],
            device_id={"tp": far}, device_id_type=MESH,
        )

    def y_out(j):
        return pltpu.make_async_copy(
            xb.at[pl.ds(two + rows, rows), pl.ds(al(j * wide, wide), wide)],
            y_ref.at[:, pl.ds(al(j * wide, wide), wide)],
            ysem.at[j],
        )

    own = pltpu.make_async_copy(x_ref, xb.at[pl.ds(0, rows), :], xsem)
    own.start()
    fetch_gu(0, 0)

    barrier = pltpu.get_barrier_semaphore()
    for peer in (sib, far):
        pl.semaphore_signal(barrier, inc=1, device_id={"tp": peer}, device_id_type=MESH)
    pl.semaphore_wait(barrier, 2)
    x_sib().start()
    for c in range(pieces):
        x_link(c).start()
    gs[...] = jnp.zeros_like(gs)
    us[...] = jnp.zeros_like(us)

    def gated(g, u):
        return (jax.nn.gelu(g) * u).astype(jnp.bfloat16)

    def flush(base, tile):
        hb[pl.ds(base, two), pl.ds(al(tile * NT, NT), NT)] = gated(gs[:two, :], us[...])

    def gate_up_half(base, half, pair, wait):
        r0 = al(base + half * rows, rows)
        for k in range(UN):
            if wait:
                wait_w(2 * pair, k)
                wait_w(2 * pair + 1, k)
            g = dot(xb[pl.ds(r0, rows), :], wr[2 * pair, k])
            u = dot(xb[pl.ds(r0, rows), :], wr[2 * pair + 1, k])
            if k < UN - 1:
                hb[pl.ds(r0, rows), k * NT:(k + 1) * NT] = gated(g, u)
            else:
                gs[half * rows:(half + 1) * rows, :] = g
                us[half * rows:(half + 1) * rows, :] = u

    def gu_pass(p, carry):
        base = al(p * two, two)
        first = p * trips

        @pl.when(p == 0)
        def _():
            own.wait()

        @pl.when(p == 1)
        def _():
            x_link(pieces - 1).wait_recv()
            x_fwd(pieces - 1).start()

        pair0 = lax.rem(first, 2)
        fetch_gu(1, 1 - pair0)
        flush(al((1 - p) * two, two), tiles - 1)
        gate_up_half(base, 0, pair0, True)

        @pl.when(p == 0)
        def _():
            x_sib().wait_recv()

        @pl.when(p == 1)
        def _():
            for c in range(pieces):
                x_fwd(c).wait_recv()

        gate_up_half(base, 1, pair0, False)

        def trip(t, carry):
            pair = lax.rem(first + t, 2)

            @pl.when(t + 1 < trips)
            def _():
                fetch_gu(t + 1, 1 - pair)

            @pl.when(jnp.logical_and(t + 1 == trips, p == 0))
            def _():
                fetch_gu(0, 1 - pair)

            @pl.when(jnp.logical_and(t + 1 == trips, p == 1))
            def _():
                fetch_d(0, 0)
                fetch_d(1, 1)

            @pl.when(jnp.logical_and(t > 1, p == 0))
            def _():
                x_link(t - 2).wait_recv()
                x_fwd(t - 2).start()

            @pl.when(jnp.logical_and(t + 1 == trips, p == 0))
            def _():
                x_link(pieces - 2).wait_recv()
                x_fwd(pieces - 2).start()

            for k in range(UN):
                wait_w(2 * pair, k)
                wait_w(2 * pair + 1, k)
            flush(base, t * UN - 1)
            for k in range(UN):
                g = dot(xb[pl.ds(base, two), :], wr[2 * pair, k])
                u = dot(xb[pl.ds(base, two), :], wr[2 * pair + 1, k])
                if k < UN - 1:
                    hb[pl.ds(base, two), pl.ds(al((t * UN + k) * NT, NT), NT)] = gated(g, u)
                else:
                    gs[:two, :] = g
                    us[...] = u
            return carry

        lax.fori_loop(1, trips, trip, 0)
        return carry

    lax.fori_loop(0, 2, gu_pass, 0)
    flush(two, tiles - 1)
    for c in range(pieces):
        x_fwd(c).wait_send()

    def down(d, carry):
        r = d // trips
        j = lax.rem(d, trips)
        half = lax.rem(d, 4)
        base = al((1 - r) * two, two)

        @pl.when(d + 2 < 2 * trips)
        def _():
            fetch_d(lax.rem(d + 2, trips), lax.rem(d + 2, 4))

        for k in range(UN):
            wait_w(half, k)
        for k in range(UN):
            term = dot(hb[pl.ds(base + rows, rows), :], wr[half, k])
            xb[pl.ds(al(r * two, two), rows), pl.ds(al(j * wide + k * NT, NT), NT)] = term.astype(jnp.bfloat16)
        t_sib(r, j).start()
        for k in range(UN):
            gs[k * rows:(k + 1) * rows, :] = dot(hb[pl.ds(base, rows), :], wr[half, k])
        t_sib(r, j).wait_recv()

        @pl.when(r == 0)
        def _():
            for k in range(UN):
                cols = pl.ds(al(j * wide + k * NT, NT), NT)
                total = gs[k * rows:(k + 1) * rows, :] + sib_in[:, cols].astype(jnp.float32)
                xb[pl.ds(rows, rows), cols] = total.astype(jnp.bfloat16)
            t_link(j).start()

        @pl.when(r == 1)
        def _():
            t_link(j).wait_recv()
            for k in range(UN):
                cols = pl.ds(al(j * wide + k * NT, NT), NT)
                total = gs[k * rows:(k + 1) * rows, :] + sib_in[:, cols].astype(jnp.float32)
                total = total + link_in[:, cols].astype(jnp.float32)
                xb[pl.ds(two + rows, rows), cols] = total.astype(jnp.bfloat16)
            y_out(j).start()

        return carry

    lax.fori_loop(0, 2 * trips, down, 0)

    x_sib().wait_send()
    for c in range(pieces):
        x_link(c).wait_send()
    for j in range(trips):
        t_sib(0, j).wait_send()
        t_sib(1, j).wait_send()
        t_link(j).wait_send()
        y_out(j).wait()


def block(x, w_gate, w_up, w_down):
    rows, depth = x.shape
    trips = depth // NT // UN
    pieces = 7
    any_spec = pl.BlockSpec(memory_space=pl.ANY)
    dma = pltpu.SemaphoreType.DMA
    return pl.pallas_call(
        kernel,
        out_shape=jax.ShapeDtypeStruct((rows, depth), jnp.bfloat16),
        in_specs=[any_spec] * 4,
        out_specs=any_spec,
        scratch_shapes=[
            pltpu.VMEM((4 * rows, depth), jnp.bfloat16),
            pltpu.VMEM((4 * rows, depth), jnp.bfloat16),
            pltpu.VMEM((4, UN, depth, NT), jnp.bfloat16),
            pltpu.VMEM((UN * rows, NT), jnp.float32),
            pltpu.VMEM((2 * rows, NT), jnp.float32),
            pltpu.VMEM((rows, depth), jnp.bfloat16),
            pltpu.VMEM((rows, depth), jnp.bfloat16),
            dma((4, UN)),
            dma,
            dma,
            dma,
            dma((pieces,)),
            dma((pieces,)),
            dma((pieces,)),
            dma((pieces,)),
            dma((2, trips)),
            dma((2, trips)),
            dma((trips,)),
            dma((trips,)),
            dma((trips,)),
        ],
        compiler_params=pltpu.CompilerParams(
            collective_id=0, has_side_effects=True, vmem_limit_bytes=VMEM_LIMIT
        ),
    )(x, w_gate, w_up, w_down)


def solution(mesh):
    return jax.shard_map(
        block,
        mesh=mesh,
        in_specs=(P(("dp", "tp"), None), P(None, "tp"), P(None, "tp"), P("tp", None)),
        out_specs=P(("dp", "tp"), None),
        check_vma=False,
    )
```

time: 340 us -> 196 us (0.58)
  Pallas kernels: 0 us -> 193 us
  matrix products: 186 us -> 0 us
  waiting for transfers between devices: 141 us -> 0 us
  between operations: 13.4 us -> 0.01 us
    pallas_call x0 -> x1, Pallas kernels: none -> 193 us  [block(): pl.pallas_call(kernel, out_shape=jax.ShapeDtypeStruct((rows, depth), jnp....]
    dot_general x3 -> x0, matrix products: 186 us -> none  [the longest x1 63.6 us: step(): gate = jnp.dot(rows, w_gate, preferred_element_type=jnp.float32)]
    reduce_scatter x1 -> x0, waiting for transfers between devices: 72.8 us -> none  [step(): return lax.psum_scatter(term, 'tp', scatter_dimension=0, tiled=True)]
    all_gather x1 -> x0, waiting for transfers between devices: 67.3 us -> none  [step(): rows = lax.all_gather(x, 'tp', axis=0, tiled=True)]
  transfers between devices with their start and end apart: 2 -> 0, of which waited for: 2 -> 0; matrix products, arithmetic and copies ran while one was open for 0% -> 0% of each run, Pallas kernels for 0% -> 0%
where the time goes in v1:
time: 196 us
  Pallas kernels  193 us (98%)
  local copies, waits for them, and re-layouts  3.26 us (2%)
    pallas_call x1, Pallas kernels, block(): pl.pallas_call(kernel, out_shape=jax.ShapeDtypeStruct((rows, depth), jnp....  193 us

profile of v1, /device:TPU:0, one launch (start us, length us, event | category | flops | bytes accessed | tf_op | source)
XLA Modules:
  0.0 196.2 jit_solution(8511042970649303434)
XLA Ops:
  0.0 192.9 %shard_map.46 = bf16[224,5376]{1,0:T(8,128)(2,1)} custom-call(bf16[224,5376]{1,0:T(8,128)(2,1)} %x_ref.1, bf16[5376,5376]{1,0:T(8,128)(2,1)} %wg_ref.1, bf16[5376,5376]{1,0:T(8,128)(2,1)} %wu_ref.1, bf16[5376,5376]{1,0:T(8,128)(2,1)} %wd_ref.1), custom_call_target="tpu_custom_call" | custom-call | tf_op jit(solution)/shard_map/pallas_call | solution.py:273
  192.9 3.3 %copy.6 = bf16[224,5376]{1,0:T(8,128)(2,1)} copy(bf16[224,5376]{1,0:T(8,128)(2,1)} %shard_map.46) | data formatting | bytes 4816896

commit v2 on v1

v2 whole, which is shorter than its diff:
```python
import functools

import jax
import jax.numpy as jnp
from jax import lax
from jax.experimental import pallas as pl
from jax.experimental.pallas import tpu as pltpu
from jax.sharding import PartitionSpec as P

NT = 256
UN = 3
SLOTS = 4 * UN
AHEAD = 3 * UN
VMEM_LIMIT = 67043328
MESH = pl.DeviceIdType.MESH


def dot(a, b):
    return jnp.dot(a, b, preferred_element_type=jnp.float32)


def kernel(
    x_ref, wg_ref, wu_ref, wd_ref, y_ref,
    xb, hb, wr, gs, sib_in, link_in,
    wsem, xsem, xsib_send, xsib_recv, xlink_send, xlink_recv, fwd_send, fwd_recv,
    sib_send, sib_recv, link_send, link_recv, ysem,
):
    rows, depth = x_ref.shape
    two = 2 * rows
    tiles = depth // NT
    trips = tiles // UN
    wide = UN * NT
    pieces = xlink_recv.shape[0]
    prow = rows // pieces

    me = lax.axis_index("tp")
    sib = me + 1 - 2 * lax.rem(me, 2)
    far = lax.rem(me + 2, 4)

    def al(v, m):
        return pl.multiple_of(v, m)

    def tile_copy(w, slot, tile):
        return pltpu.make_async_copy(
            w.at[:, pl.ds(al(tile * NT, NT), NT)], wr.at[slot], wsem.at[slot]
        )

    def fetch_gu(t, pair):
        for k in range(UN):
            tile_copy(wg_ref, (2 * pair) * UN + k, t * UN + k).start()
            tile_copy(wu_ref, (2 * pair + 1) * UN + k, t * UN + k).start()

    def wait_w(slot):
        tile_copy(wg_ref, slot, 0).wait()

    def fetch_d(q):
        tile_copy(wd_ref, lax.rem(q, SLOTS), lax.rem(q, tiles)).start()

    def x_sib():
        return pltpu.make_async_remote_copy(
            src_ref=x_ref, dst_ref=xb.at[pl.ds(rows, rows), :],
            send_sem=xsib_send, recv_sem=xsib_recv,
            device_id={"tp": sib}, device_id_type=MESH,
        )

    def x_link(c):
        return pltpu.make_async_remote_copy(
            src_ref=x_ref.at[pl.ds(c * prow, prow), :],
            dst_ref=xb.at[pl.ds(two + c * prow, prow), :],
            send_sem=xlink_send.at[c], recv_sem=xlink_recv.at[c],
            device_id={"tp": far}, device_id_type=MESH,
        )

    def x_fwd(c):
        return pltpu.make_async_remote_copy(
            src_ref=xb.at[pl.ds(two + c * prow, prow), :],
            dst_ref=xb.at[pl.ds(two + rows + c * prow, prow), :],
            send_sem=fwd_send.at[c], recv_sem=fwd_recv.at[c],
            device_id={"tp": sib}, device_id_type=MESH,
        )

    def t_sib(r, i, tile, n):
        cols = pl.ds(al(tile * NT, NT), n * NT)
        return pltpu.make_async_remote_copy(
            src_ref=xb.at[pl.ds(al(r * two, two), rows), cols],
            dst_ref=sib_in.at[:, cols],
            send_sem=sib_send.at[i], recv_sem=sib_recv.at[i],
            device_id={"tp": sib}, device_id_type=MESH,
        )

    def t_link(i, tile, n):
        cols = pl.ds(al(tile * NT, NT), n * NT)
        return pltpu.make_async_remote_copy(
            src_ref=xb.at[pl.ds(rows, rows), cols],
            dst_ref=link_in.at[:, cols],
            send_sem=link_send.at[i], recv_sem=link_recv.at[i],
            device_id={"tp": far}, device_id_type=MESH,
        )

    def y_out(tile):
        cols = pl.ds(al(tile * NT, NT), NT)
        return pltpu.make_async_copy(
            xb.at[pl.ds(two + rows, rows), cols], y_ref.at[:, cols], ysem.at[tile]
        )

    own = pltpu.make_async_copy(x_ref, xb.at[pl.ds(0, rows), :], xsem)
    own.start()
    fetch_gu(0, 0)

    barrier = pltpu.get_barrier_semaphore()
    for peer in (sib, far):
        pl.semaphore_signal(barrier, inc=1, device_id={"tp": peer}, device_id_type=MESH)
    pl.semaphore_wait(barrier, 2)
    x_sib().start()
    for c in range(pieces):
        x_link(c).start()
    gs[...] = jnp.zeros_like(gs)

    def gated(g, u):
        return (jax.nn.gelu(g) * u).astype(jnp.bfloat16)

    def flush(base, tile):
        hb[pl.ds(base, two), pl.ds(al(tile * NT, NT), NT)] = gated(gs[0, :two, :], gs[1, :two, :])

    def gate_up_half(base, half, pair, wait):
        r0 = al(base + half * rows, rows)
        for k in range(UN):
            if wait:
                wait_w(2 * pair * UN + k)
                wait_w((2 * pair + 1) * UN + k)
            g = dot(xb[pl.ds(r0, rows), :], wr[2 * pair * UN + k])
            u = dot(xb[pl.ds(r0, rows), :], wr[(2 * pair + 1) * UN + k])
            if k < UN - 1:
                hb[pl.ds(r0, rows), k * NT:(k + 1) * NT] = gated(g, u)
            else:
                gs[0, half * rows:(half + 1) * rows, :] = g
                gs[1, half * rows:(half + 1) * rows, :] = u

    def gu_pass(p, carry):
        base = al(p * two, two)
        first = p * trips

        @pl.when(p == 0)
        def _():
            own.wait()

        @pl.when(p == 1)
        def _():
            x_link(pieces - 1).wait_recv()
            x_fwd(pieces - 1).start()

        pair0 = lax.rem(first, 2)
        fetch_gu(1, 1 - pair0)
        flush(al((1 - p) * two, two), tiles - 1)
        gate_up_half(base, 0, pair0, True)

        @pl.when(p == 0)
        def _():
            x_sib().wait_recv()

        @pl.when(p == 1)
        def _():
            for c in range(pieces):
                x_fwd(c).wait_recv()

        gate_up_half(base, 1, pair0, False)

        def trip(t, carry):
            pair = lax.rem(first + t, 2)

            @pl.when(t + 1 < trips)
            def _():
                fetch_gu(t + 1, 1 - pair)

            @pl.when(jnp.logical_and(t + 1 == trips, p == 0))
            def _():
                fetch_gu(0, 1 - pair)

            @pl.when(jnp.logical_and(t + 1 == trips, p == 1))
            def _():
                for q in range(SLOTS // 2):
                    fetch_d(q)

            @pl.when(jnp.logical_and(t > 1, p == 0))
            def _():
                x_link(t - 2).wait_recv()
                x_fwd(t - 2).start()

            @pl.when(jnp.logical_and(t + 1 == trips, p == 0))
            def _():
                x_link(pieces - 2).wait_recv()
                x_fwd(pieces - 2).start()

            for k in range(UN):
                wait_w(2 * pair * UN + k)
                wait_w((2 * pair + 1) * UN + k)
            flush(base, t * UN - 1)
            for k in range(UN):
                g = dot(xb[pl.ds(base, two), :], wr[2 * pair * UN + k])
                u = dot(xb[pl.ds(base, two), :], wr[(2 * pair + 1) * UN + k])
                if k < UN - 1:
                    hb[pl.ds(base, two), pl.ds(al((t * UN + k) * NT, NT), NT)] = gated(g, u)
                else:
                    gs[0, :two, :] = g
                    gs[1, :two, :] = u
            return carry

        lax.fori_loop(1, trips, trip, 0)
        return carry

    lax.fori_loop(0, 2, gu_pass, 0)
    flush(two, tiles - 1)
    for c in range(pieces):
        x_fwd(c).wait_send()

    for q in range(SLOTS // 2, AHEAD):
        fetch_d(q)

    many = tiles // UN - 1
    half = many + UN

    def spot(i):
        j = lax.rem(i, half)
        few_first = jnp.where(j < UN, j, (j - UN + 1) * UN)
        few_last = jnp.where(j < many, j * UN, many * UN + j - many)
        return jnp.where(i < half, few_first, few_last)

    def finish(i, r, n):
        tile = spot(i)
        t_sib(r, i, tile, n).wait_recv()
        if r == 1:
            if n == UN:
                for m in range(UN):
                    pl.when(tile == 0)(lambda m=m: t_link(m, m, 1).wait_recv())
                pl.when(tile > 0)(lambda: t_link(UN - 1 + tile // UN, tile, UN).wait_recv())
            else:
                pl.when(tile == many * UN)(lambda: t_link(half - 1, tile, UN).wait_recv())
        buf = lax.rem(i, 2)
        for k in range(n):
            cols = pl.ds(al((tile + k) * NT, NT), NT)
            total = gs[buf, k * rows:(k + 1) * rows, :] + sib_in[:, cols].astype(jnp.float32)
            if r == 0:
                xb[pl.ds(rows, rows), cols] = total.astype(jnp.bfloat16)
            else:
                total = total + link_in[:, cols].astype(jnp.float32)
                xb[pl.ds(two + rows, rows), cols] = total.astype(jnp.bfloat16)
        if r == 0:
            t_link(i, tile, n).start()
        else:
            for k in range(n):
                y_out(tile + k).start()

    def matmuls(i, r, n):
        tile = spot(i)
        base = al((1 - r) * two, two)
        first = r * tiles + tile
        buf = lax.rem(i, 2)
        for k in range(n):
            slot = lax.rem(first + k, SLOTS)
            term = dot(hb[pl.ds(base + rows, rows), :], wr[slot])
            xb[pl.ds(al(r * two, two), rows), pl.ds(al((tile + k) * NT, NT), NT)] = term.astype(jnp.bfloat16)
            gs[buf, k * rows:(k + 1) * rows, :] = dot(hb[pl.ds(base, rows), :], wr[slot])

    def weights(i, r, n):
        first = r * tiles + spot(i)
        for k in range(n):

            @pl.when(first + AHEAD + k < 2 * tiles)
            def _():
                fetch_d(first + AHEAD + k)

        for k in range(n):
            wait_w(lax.rem(first + k, SLOTS))

    def few_first(i, carry):
        weights(i, 0, 1)

        @pl.when(i >= 2)
        def _():
            finish(i - 2, 0, 1)

        @pl.when(i >= 1)
        def _():
            t_sib(0, i - 1, spot(i - 1), 1).start()

        matmuls(i, 0, 1)
        return carry

    def middle(i, carry):
        r = i // half
        weights(i, r, UN)
        pl.when(i < UN + 2)(lambda: finish(i - 2, 0, 1))
        pl.when(jnp.logical_and(i >= UN + 2, i < half + 2))(lambda: finish(i - 2, 0, UN))
        pl.when(i >= half + 2)(lambda: finish(i - 2, 1, UN))
        pl.when(i == UN)(lambda: t_sib(0, i - 1, spot(i - 1), 1).start())
        pl.when(i > UN)(lambda: t_sib((i - 1) // half, i - 1, spot(i - 1), UN).start())
        matmuls(i, r, UN)
        return carry

    def few_last(i, carry):
        weights(i, 1, 1)
        pl.when(i < half + many + 2)(lambda: finish(i - 2, 1, UN))
        pl.when(i >= half + many + 2)(lambda: finish(i - 2, 1, 1))
        pl.when(i == half + many)(lambda: t_sib(1, i - 1, spot(i - 1), UN).start())
        pl.when(i > half + many)(lambda: t_sib(1, i - 1, spot(i - 1), 1).start())
        matmuls(i, 1, 1)
        return carry

    lax.fori_loop(0, UN, few_first, 0)
    lax.fori_loop(UN, half + many, middle, 0)
    lax.fori_loop(half + many, 2 * half, few_last, 0)
    t_sib(1, 2 * half - 1, tiles - 1, 1).start()
    finish(2 * half - 2, 1, 1)
    finish(2 * half - 1, 1, 1)

    x_sib().wait_send()
    for c in range(pieces):
        x_link(c).wait_send()
    for i in range(UN):
        t_sib(0, i, i, 1).wait_send()
        t_link(i, i, 1).wait_send()
        t_sib(1, half + many + i, many * UN + i, 1).wait_send()
    for i in range(many):
        t_sib(0, UN + i, (i + 1) * UN, UN).wait_send()
        t_link(UN + i, (i + 1) * UN, UN).wait_send()
        t_sib(1, half + i, i * UN, UN).wait_send()
    for tile in range(tiles):
        y_out(tile).wait()


def block(x, w_gate, w_up, w_down):
    rows, depth = x.shape
    tiles = depth // NT
    half = tiles // UN - 1 + UN
    pieces = 7
    any_spec = pl.BlockSpec(memory_space=pl.ANY)
    dma = pltpu.SemaphoreType.DMA
    return pl.pallas_call(
        kernel,
        out_shape=jax.ShapeDtypeStruct((rows, depth), jnp.bfloat16),
        in_specs=[any_spec] * 4,
        out_specs=any_spec,
        scratch_shapes=[
            pltpu.VMEM((4 * rows, depth), jnp.bfloat16),
            pltpu.VMEM((4 * rows, depth), jnp.bfloat16),
            pltpu.VMEM((SLOTS, depth, NT), jnp.bfloat16),
            pltpu.VMEM((2, UN * rows, NT), jnp.float32),
            pltpu.VMEM((rows, depth), jnp.bfloat16),
            pltpu.VMEM((rows, depth), jnp.bfloat16),
            dma((SLOTS,)),
            dma,
            dma,
            dma,
            dma((pieces,)),
            dma((pieces,)),
            dma((pieces,)),
            dma((pieces,)),
            dma((2 * half,)),
            dma((2 * half,)),
            dma((half,)),
            dma((half,)),
            dma((tiles,)),
        ],
        compiler_params=pltpu.CompilerParams(
            collective_id=0, has_side_effects=True, vmem_limit_bytes=VMEM_LIMIT
        ),
    )(x, w_gate, w_up, w_down)


def solution(mesh):
    return jax.shard_map(
        block,
        mesh=mesh,
        in_specs=(P(("dp", "tp"), None), P(None, "tp"), P(None, "tp"), P("tp", None)),
        out_specs=P(("dp", "tp"), None),
        check_vma=False,
    )
```

time: 196 us -> 183 us (0.934)
  Pallas kernels: 193 us -> 180 us
    pallas_call x1, Pallas kernels: 193 us -> 180 us  [block(): pl.pallas_call(kernel, out_shape=jax.ShapeDtypeStruct((rows, depth), jnp....]
where the time goes in v2:
time: 183 us
  Pallas kernels  180 us (98%)
  local copies, waits for them, and re-layouts  3.26 us (2%)
    pallas_call x1, Pallas kernels, block(): pl.pallas_call(kernel, out_shape=jax.ShapeDtypeStruct((rows, depth), jnp....  180 us

profile of v2, /device:TPU:0, one launch (start us, length us, event | category | flops | bytes accessed | tf_op | source)
XLA Modules:
  0.0 182.9 jit_solution(15901057120091706365)
XLA Ops:
  0.0 179.6 %shard_map.46 = bf16[224,5376]{1,0:T(8,128)(2,1)} custom-call(bf16[224,5376]{1,0:T(8,128)(2,1)} %x_ref.1, bf16[5376,5376]{1,0:T(8,128)(2,1)} %wg_ref.1, bf16[5376,5376]{1,0:T(8,128)(2,1)} %wu_ref.1, bf16[5376,5376]{1,0:T(8,128)(2,1)} %wd_ref.1), custom_call_target="tpu_custom_call" | custom-call | tf_op jit(solution)/shard_map/pallas_call | solution.py:338
  179.6 3.3 %copy.6 = bf16[224,5376]{1,0:T(8,128)(2,1)} copy(bf16[224,5376]{1,0:T(8,128)(2,1)} %shard_map.46) | data formatting | bytes 4816896

commit v3 on v2

--- a/solution.py
+++ b/solution.py
@@ -45,8 +45,8 @@
             w.at[:, pl.ds(al(tile * NT, NT), NT)], wr.at[slot], wsem.at[slot]
         )
 
-    def fetch_gu(t, pair):
-        for k in range(UN):
+    def fetch_gu(t, pair, ks=range(UN)):
+        for k in ks:
             tile_copy(wg_ref, (2 * pair) * UN + k, t * UN + k).start()
             tile_copy(wu_ref, (2 * pair + 1) * UN + k, t * UN + k).start()
 
@@ -105,7 +105,7 @@
 
     own = pltpu.make_async_copy(x_ref, xb.at[pl.ds(0, rows), :], xsem)
     own.start()
-    fetch_gu(0, 0)
+    fetch_gu(0, 0, range(2))
 
     barrier = pltpu.get_barrier_semaphore()
     for peer in (sib, far):
@@ -122,12 +122,16 @@
     def flush(base, tile):
         hb[pl.ds(base, two), pl.ds(al(tile * NT, NT), NT)] = gated(gs[0, :two, :], gs[1, :two, :])
 
-    def gate_up_half(base, half, pair, wait):
+    def gate_up_half(base, half, pair):
         r0 = al(base + half * rows, rows)
         for k in range(UN):
-            if wait:
+            if half == 0:
                 wait_w(2 * pair * UN + k)
                 wait_w((2 * pair + 1) * UN + k)
+                if k == 0:
+                    pl.when(base == 0)(lambda: fetch_gu(0, pair, range(2, UN)))
+                else:
+                    fetch_gu(1, 1 - pair, range(1) if k == 1 else range(1, UN))
             g = dot(xb[pl.ds(r0, rows), :], wr[2 * pair * UN + k])
             u = dot(xb[pl.ds(r0, rows), :], wr[(2 * pair + 1) * UN + k])
             if k < UN - 1:
@@ -150,9 +154,8 @@
             x_fwd(pieces - 1).start()
 
         pair0 = lax.rem(first, 2)
-        fetch_gu(1, 1 - pair0)
         flush(al((1 - p) * two, two), tiles - 1)
-        gate_up_half(base, 0, pair0, True)
+        gate_up_half(base, 0, pair0)
 
         @pl.when(p == 0)
         def _():
@@ -163,7 +166,7 @@
             for c in range(pieces):
                 x_fwd(c).wait_recv()
 
-        gate_up_half(base, 1, pair0, False)
+        gate_up_half(base, 1, pair0)
 
         def trip(t, carry):
             pair = lax.rem(first + t, 2)
@@ -225,7 +228,7 @@
         few_last = jnp.where(j < many, j * UN, many * UN + j - many)
         return jnp.where(i < half, few_first, few_last)
 
-    def finish(i, r, n):
+    def finish(i, r, n, at=0):
         tile = spot(i)
         t_sib(r, i, tile, n).wait_recv()
         if r == 1:
@@ -238,7 +241,7 @@
         buf = lax.rem(i, 2)
         for k in range(n):
             cols = pl.ds(al((tile + k) * NT, NT), NT)
-            total = gs[buf, k * rows:(k + 1) * rows, :] + sib_in[:, cols].astype(jnp.float32)
+            total = gs[buf, (at + k) * rows:(at + k + 1) * rows, :] + sib_in[:, cols].astype(jnp.float32)
             if r == 0:
                 xb[pl.ds(rows, rows), cols] = total.astype(jnp.bfloat16)
             else:
@@ -250,7 +253,7 @@
             for k in range(n):
                 y_out(tile + k).start()
 
-    def matmuls(i, r, n):
+    def matmuls(i, r, n, at=0):
         tile = spot(i)
         base = al((1 - r) * two, two)
         first = r * tiles + tile
@@ -259,7 +262,7 @@
             slot = lax.rem(first + k, SLOTS)
             term = dot(hb[pl.ds(base + rows, rows), :], wr[slot])
             xb[pl.ds(al(r * two, two), rows), pl.ds(al((tile + k) * NT, NT), NT)] = term.astype(jnp.bfloat16)
-            gs[buf, k * rows:(k + 1) * rows, :] = dot(hb[pl.ds(base, rows), :], wr[slot])
+            gs[buf, pl.ds((at + k) * rows, rows), :] = dot(hb[pl.ds(base, rows), :], wr[slot])
 
     def weights(i, r, n):
         first = r * tiles + spot(i)
@@ -300,18 +303,17 @@
     def few_last(i, carry):
         weights(i, 1, 1)
         pl.when(i < half + many + 2)(lambda: finish(i - 2, 1, UN))
-        pl.when(i >= half + many + 2)(lambda: finish(i - 2, 1, 1))
         pl.when(i == half + many)(lambda: t_sib(1, i - 1, spot(i - 1), UN).start())
         pl.when(i > half + many)(lambda: t_sib(1, i - 1, spot(i - 1), 1).start())
-        matmuls(i, 1, 1)
+        matmuls(i, 1, 1, jnp.where(i == 2 * half - 1, 1, 0))
         return carry
 
     lax.fori_loop(0, UN, few_first, 0)
     lax.fori_loop(UN, half + many, middle, 0)
     lax.fori_loop(half + many, 2 * half, few_last, 0)
     t_sib(1, 2 * half - 1, tiles - 1, 1).start()
-    finish(2 * half - 2, 1, 1)
-    finish(2 * half - 1, 1, 1)
+    for i in range(half + many, 2 * half):
+        finish(i, 1, 1, i // (2 * half - 1))
 
     x_sib().wait_send()
     for c in range(pieces):

time: 183 us -> 180 us (0.984)
  Pallas kernels: 180 us -> 176 us
    pallas_call x1, Pallas kernels: 180 us -> 176 us  [block(): pl.pallas_call(kernel, out_shape=jax.ShapeDtypeStruct((rows, depth), jnp....]
where the time goes in v3:
time: 180 us; the launch traced here: 179 us
  Pallas kernels  176 us (98%)
  local copies, waits for them, and re-layouts  3.26 us (2%)
    pallas_call x1, Pallas kernels, block(): pl.pallas_call(kernel, out_shape=jax.ShapeDtypeStruct((rows, depth), jnp....  176 us

profile of v3, /device:TPU:0, one launch (start us, length us, event | category | flops | bytes accessed | tf_op | source)
XLA Modules:
  0.0 179.5 jit_solution(10603790230576674231)
XLA Ops:
  0.0 176.2 %shard_map.46 = bf16[224,5376]{1,0:T(8,128)(2,1)} custom-call(bf16[224,5376]{1,0:T(8,128)(2,1)} %x_ref.1, bf16[5376,5376]{1,0:T(8,128)(2,1)} %wg_ref.1, bf16[5376,5376]{1,0:T(8,128)(2,1)} %wu_ref.1, bf16[5376,5376]{1,0:T(8,128)(2,1)} %wd_ref.1), custom_call_target="tpu_custom_call" | custom-call | tf_op jit(solution)/shard_map/pallas_call | solution.py:340
  176.2 3.3 %copy.6 = bf16[224,5376]{1,0:T(8,128)(2,1)} copy(bf16[224,5376]{1,0:T(8,128)(2,1)} %shard_map.46) | data formatting | bytes 4816896

commit v4 on v3

--- a/solution.py
+++ b/solution.py
@@ -171,28 +171,21 @@
         def trip(t, carry):
             pair = lax.rem(first + t, 2)
 
-            @pl.when(t + 1 < trips)
+            ends = jnp.logical_and(t + 1 == trips, p == 1)
+
+            @pl.when(jnp.logical_not(ends))
             def _():
-                fetch_gu(t + 1, 1 - pair)
-
-            @pl.when(jnp.logical_and(t + 1 == trips, p == 0))
-            def _():
-                fetch_gu(0, 1 - pair)
-
-            @pl.when(jnp.logical_and(t + 1 == trips, p == 1))
+                fetch_gu(lax.rem(t + 1, trips), 1 - pair)
+
+            @pl.when(ends)
             def _():
                 for q in range(SLOTS // 2):
                     fetch_d(q)
 
-            @pl.when(jnp.logical_and(t > 1, p == 0))
+            @pl.when(p == 0)
             def _():
-                x_link(t - 2).wait_recv()
-                x_fwd(t - 2).start()
-
-            @pl.when(jnp.logical_and(t + 1 == trips, p == 0))
-            def _():
-                x_link(pieces - 2).wait_recv()
-                x_fwd(pieces - 2).start()
+                x_link(t - 1).wait_recv()
+                x_fwd(t - 1).start()
 
             for k in range(UN):
                 wait_w(2 * pair * UN + k)
@@ -369,9 +362,43 @@
     )(x, w_gate, w_up, w_down)
 
 
+def hand_over(src, dst, buf, arrived, left):
+    pieces = arrived.shape[0]
+    prow = src.shape[0] // pieces
+
+    def part(c, a, b, sem):
+        span = pl.ds(c * prow, prow)
+        return pltpu.make_async_copy(a.at[span, :], b.at[span, :], sem.at[c])
+
+    for c in range(pieces):
+        part(c, src, buf, arrived).start()
+    for c in range(pieces):
+        part(c, src, buf, arrived).wait()
+        part(c, buf, dst, left).start()
+    for c in range(pieces):
+        part(c, buf, dst, left).wait()
+
+
+def step(x, w_gate, w_up, w_down):
+    y = block(x, w_gate, w_up, w_down)
+    any_spec = pl.BlockSpec(memory_space=pl.ANY)
+    return pl.pallas_call(
+        hand_over,
+        out_shape=jax.ShapeDtypeStruct(y.shape, y.dtype),
+        in_specs=[any_spec],
+        out_specs=any_spec,
+        scratch_shapes=[
+            pltpu.VMEM(y.shape, y.dtype),
+            pltpu.SemaphoreType.DMA((14,)),
+            pltpu.SemaphoreType.DMA((14,)),
+        ],
+        compiler_params=pltpu.CompilerParams(vmem_limit_bytes=VMEM_LIMIT),
+    )(y)
+
+
 def solution(mesh):
     return jax.shard_map(
-        block,
+        step,
         mesh=mesh,
         in_specs=(P(("dp", "tp"), None), P(None, "tp"), P(None, "tp"), P("tp", None)),
         out_specs=P(("dp", "tp"), None),

time: 180 us -> 179 us (level)
  local copies, waits for them, and re-layouts: 3.26 us -> 0 us
  Pallas kernels: 176 us -> 179 us
    unnamed x1 -> x0, local copies, waits for them, and re-layouts: 3.26 us -> none
    pallas_call x0 -> x1, Pallas kernels: none -> 2.68 us  [step(): pl.pallas_call(hand_over, out_shape=jax.ShapeDtypeStruct(y.shape, y.dtype...]
where the time goes in v4:
time: 179 us
  Pallas kernels  179 us (100%)
    pallas_call x1, Pallas kernels, block(): pl.pallas_call(kernel, out_shape=jax.ShapeDtypeStruct((rows, depth), jnp....  176 us

profile of v4, /device:TPU:0, one launch (start us, length us, event | category | flops | bytes accessed | tf_op | source)
XLA Modules:
  0.0 178.9 jit_solution(1234333251192560996)
XLA Ops:
  0.0 176.1 %shard_map.46.src = bf16[224,5376]{1,0:T(8,128)(2,1)} custom-call(bf16[224,5376]{1,0:T(8,128)(2,1)} %x_ref.1, bf16[5376,5376]{1,0:T(8,128)(2,1)} %wg_ref.1, bf16[5376,5376]{1,0:T(8,128)(2,1)} %wu_ref.1, bf16[5376,5376]{1,0:T(8,128)(2,1)} %wd_ref.1), custom_call_target="tpu_custom_call" | custom-call | tf_op jit(solution)/shard_map/pallas_call | solution.py:333
  176.1 2.7 %shard_map.47 = bf16[224,5376]{1,0:T(8,128)(2,1)} custom-call(bf16[224,5376]{1,0:T(8,128)(2,1)} %shard_map.46.src), custom_call_target="tpu_custom_call" | custom-call | tf_op jit(solution)/shard_map/pallas_call | solution.py:385
